TPU v7x, 128 devices: a whole 4x4x4 slice. The times are simulated.
128 devices in a mesh: owner: 8 (over y, core), rows: 16 (over z, x).
Axes of the slice: x: 4, y: 4, z: 4, core: 2. Of those that a mesh axis runs over, the one named last changes fastest.
Arguments:
- train_gate: float32 [64, 2048, 1024], P('owner', 'rows'), may hold values from -0.1875 to 0.1875
- other_gate: bfloat16 [64, 2048, 1024], P('owner', 'rows'), may hold values from -0.0625 to 0.0625
- train_up: float32 [64, 2048, 1024], P('owner', 'rows'), may hold values from -0.1875 to 0.1875
- other_up: bfloat16 [64, 2048, 1024], P('owner', 'rows'), may hold values from -0.0625 to 0.0625
- train_down: float32 [64, 1024, 2048], P('owner', None, 'rows'), may hold values from -0.25 to 0.25
- other_down: bfloat16 [64, 1024, 2048], P('owner', None, 'rows'), may hold values from -0.09375 to 0.09375
- router_weight: float32 [2048, 64], P('rows', 'owner'), may hold values from -0.125 to 0.125
- router_gain: float32 [2048], P('rows'), may hold values from 0.25 to 1.75
Outputs:
- ready_gate: bfloat16 [64, 2048, 1024], P('owner', None, 'rows')
- ready_up: bfloat16 [64, 2048, 1024], P('owner', None, 'rows')
- ready_down: bfloat16 [64, 1024, 2048], P('owner', 'rows')
- scale_gate: float32 [64, 1024], P('owner', 'rows')
- scale_up: float32 [64, 1024], P('owner', 'rows')
- scale_down: float32 [64, 1024], P('owner', 'rows')
- serve_router: bfloat16 [2048, 64], replicated
All inputs are finite; a program needn't handle non-finite values. Where the computation divides by a largest or mean magnitude, that divisor is 1e-20 or more.
Results may differ from a plain program's by a relative error of at most 0.001.
Values may be sent and summed in bfloat16 or wider, within the bound.
No kernel may reach another device: no remote copies, remote signals or barrier semaphores. Data moves between devices by JAX's collectives and lax.ppermute only.
A program may use at most 128 MiB of HBM per device.

v0:
```python
import jax
import jax.numpy as jnp
from jax import lax
from jax.sharding import PartitionSpec as P


def from_everyone(array, axis):
    peers = lax.axis_size(axis)
    return lax.all_to_all(
        jnp.broadcast_to(array[None], (peers, *array.shape)), axis, 0, 0, tiled=True
    )


def taken_together(array, axis):
    everything = from_everyone(array, axis)
    return jnp.max(everything, axis=0)


def in_one(arrays, axis):
    line, at, gathered = (jnp.concatenate([a.reshape(-1) for a in arrays]), 0, [])
    subtotal = taken_together(line, axis)
    for a in arrays:
        gathered.append(subtotal[at : at + a.size].reshape(a.shape))
        at += a.size
    return tuple(gathered)


def sent_together(arrays, axis, split_dim, concat_dim, along):
    both = jnp.concatenate(arrays, axis=along)
    filled, at, gathered = (
        lax.all_to_all(both, axis, split_axis=split_dim, concat_axis=concat_dim, tiled=True),
        0,
        [],
    )
    for a in arrays:
        gathered.append(lax.slice_in_dim(filled, at, at + a.shape[along], axis=along))
        at += a.shape[along]
    return tuple(gathered)


def in_blocks(array, dim, peers):
    before, after = (array.shape[:dim], array.shape[dim + 1 :])
    return jnp.moveaxis(array.reshape(*before, peers, -1, *after), dim, 0)


def piece_ends(length, count):
    unit = 8 if length >= 8 * count else 1
    return [length // unit * k // count * unit for k in range(1, count)]


def laid_out(tiles, dim):
    tiles = jnp.moveaxis(tiles, 0, dim)
    lengths = tiles.shape
    return tiles.reshape(*lengths[:dim], lengths[dim] * lengths[dim + 1], *lengths[dim + 2 :])


def cut_exchange(array, axis, pieces, split_dim, concat_dim):
    tiles = in_blocks(array, split_dim, lax.axis_size(axis))
    split_at = max(range(1, max(2, tiles.ndim - 1)), key=lambda d: tiles.shape[d])
    gathered = []
    for piece in jnp.split(tiles, piece_ends(tiles.shape[split_at], pieces), axis=split_at):
        if piece.size:
            gathered.append(lax.all_to_all(piece, axis, split_axis=0, concat_axis=0, tiled=True))
    return laid_out(jnp.concatenate(gathered, axis=split_at), concat_dim)


def gather_directly(array, axis, dim):
    return laid_out(from_everyone(array, axis), dim)


def shards(
    train_gate, other_gate, train_up, other_up, train_down, other_down, router_weight, router_gain
):
    latest_gate = train_gate + other_gate.astype(jnp.float32)
    latest_up = train_up + other_up.astype(jnp.float32)
    latest_down = train_down + other_down.astype(jnp.float32)
    scale_gate, scale_up, scale_down = in_one(
        (
            jnp.max(jnp.abs(latest_gate), axis=1),
            jnp.max(jnp.abs(latest_up), axis=1),
            jnp.max(jnp.abs(latest_down), axis=2),
        ),
        "rows",
    )
    narrow_gate, narrow_up, narrow_down = (
        (latest_gate / jnp.expand_dims(scale_gate, 1)).astype(jnp.bfloat16),
        (latest_up / jnp.expand_dims(scale_up, 1)).astype(jnp.bfloat16),
        (latest_down / jnp.expand_dims(scale_down, 2)).astype(jnp.bfloat16),
    )
    ready_gate, ready_up = sent_together((narrow_gate, narrow_up), "rows", 2, 1, 0)
    ready_down = cut_exchange(narrow_down, "rows", 2, 1, 2)
    scale_gate = lax.dynamic_slice_in_dim(
        scale_gate, lax.axis_index("rows") * ready_gate.shape[2], ready_gate.shape[2], axis=1
    )
    scale_up = lax.dynamic_slice_in_dim(
        scale_up, lax.axis_index("rows") * ready_up.shape[2], ready_up.shape[2], axis=1
    )
    scale_down = lax.dynamic_slice_in_dim(
        scale_down, lax.axis_index("rows") * ready_down.shape[1], ready_down.shape[1], axis=1
    )
    part_router = (router_weight * router_gain[:, None]).astype(jnp.bfloat16)
    row_router = gather_directly(part_router, "rows", 0)
    serve_router = gather_directly(row_router, "owner", 1)
    return (ready_gate, ready_up, ready_down, scale_gate, scale_up, scale_down, serve_router)


def solution(mesh):
    placed = (
        P("owner", "rows", None),
        P("owner", "rows", None),
        P("owner", "rows", None),
        P("owner", "rows", None),
        P("owner", None, "rows"),
        P("owner", None, "rows"),
        P("rows", "owner"),
        P("rows"),
    )
    return jax.shard_map(
        shards,
        mesh=mesh,
        in_specs=placed,
        out_specs=(
            P("owner", None, "rows"),
            P("owner", None, "rows"),
            P("owner", "rows", None),
            P("owner", "rows"),
            P("owner", "rows"),
            P("owner", "rows"),
            P(),
        ),
        check_vma=False,
    )
```

profile of v0, /device:TPU:1, one launch (start us, length us, event | category | flops | bytes accessed | tf_op | source)
XLA Modules:
  0.0 200.6 jit_solution(1674416194207160043)
XLA Ops:
  1.9 8.4 %all-to-all-start.4 = ((bf16[16,128,8]{1,2,0:T(8,128)(2,1)}), bf16[16,128,8]{1,2,0:T(8,128)(2,1)S(1)}, u32[]{:S(2)}, u32[]{:S(2)}) async-start(bf16[16,128,8]{1,2,0:T(8,128)(2,1)} %broadcast_in_dim.9), calls=%async_computation.4 | async-start | bytes 65536 | tf_op jit(solution)/shard_map/all_to_all | solution.py:9
  10.4 5.4 %copy.94 = f32[8,128,1024]{1,0,2:T(8,128)} copy(f32[8,128,1024]{2,1,0:T(8,128)} %param.10) | data formatting | bytes 8388608 | tf_op args[2]
  15.8 3.4 %copy.93 = bf16[8,128,1024]{1,0,2:T(8,128)(2,1)S(1)} copy(bf16[8,128,1024]{2,1,0:T(8,128)(2,1)} %param.11) | data formatting | bytes 4194304 | tf_op args[3]
  19.1 3.4 %abs_reduce_fusion.1 = f32[8,1024]{0,1:T(8,128)S(1)} fusion(f32[8,128,1024]{1,0,2:T(8,128)} %copy.94, bf16[8,128,1024]{1,0,2:T(8,128)(2,1)S(1)} %copy.93), kind=kLoop, calls=%fused_computation.6 | loop fusion | flops 4186112 | bytes 6324224 | tf_op jit(solution)/shard_map/reduce_max | solution.py:80
  22.7 5.4 %copy.91 = f32[8,128,1024]{1,0,2:T(8,128)} copy(f32[8,128,1024]{2,1,0:T(8,128)} %param.8) | data formatting | bytes 8388608 | tf_op args[0]
  28.1 4.1 %copy.90 = bf16[8,128,1024]{1,0,2:T(8,128)(2,1)} copy(bf16[8,128,1024]{2,1,0:T(8,128)(2,1)} %param.9) | data formatting | bytes 4194304 | tf_op args[1]
  32.2 4.1 %abs_reduce_fusion.2 = f32[8,1024]{0,1:T(8,128)S(1)} fusion(f32[8,128,1024]{1,0,2:T(8,128)} %copy.91, bf16[8,128,1024]{1,0,2:T(8,128)(2,1)} %copy.90), kind=kLoop, calls=%fused_computation.8 | loop fusion | flops 4186112 | bytes 6324224 | tf_op jit(solution)/shard_map/reduce_max | solution.py:79
  36.4 4.0 %abs_reduce_fusion = f32[8,1024]{1,0:T(8,128)S(1)} fusion(f32[8,1024,128]{2,1,0:T(8,128)} %param.12, bf16[8,1024,128]{2,1,0:T(8,128)(2,1)} %param.13), kind=kLoop, calls=%fused_computation.4 | loop fusion | flops 4186112 | bytes 6324224 | tf_op jit(solution)/shard_map/reduce_max | solution.py:81
  40.5 1.2 broadcast_in_dim.8
  41.7 28.0 %all_to_all.41 = f32[16,1,24576]{2,1,0:T(1,128)} all-to-all(f32[16,1,24576]{2,1,0:T(1,128)S(1)} %broadcast_in_dim.8), channel_id=1, replica_groups=mesh['owner'=8,'rows'=16] {'rows'}, dimensions={0} | all-to-all | bytes 3145728 | tf_op jit(solution)/shard_map/all_to_all | solution.py:9
  70.5 6.8 %all-to-all-start.5 = ((bf16[8,2048,8]{1,2,0:T(8,128)(2,1)}), bf16[8,2048,8]{1,2,0:T(8,128)(2,1)S(1)}, u32[]{:S(2)}, u32[]{:S(2)}) async-start(bf16[8,2048,8]{1,2,0:T(8,128)(2,1)} %broadcast_in_dim.11), calls=%async_computation.5 | async-start | bytes 524288 | tf_op jit(solution)/shard_map/all_to_all | solution.py:9
  77.3 2.4 %reduce_max.39 = f32[24576]{0:T(1024)S(1)} reduce(f32[16,1,24576]{2,1,0:T(1,128)} %all_to_all.41, f32[]{:T(128)} %constant.5.clone.1), dimensions={0,1}, to_apply=%region_3.0 | reduce | flops 368640 | bytes 1671172 | tf_op jit(solution)/shard_map/reduce_max | solution.py:16
  79.7 3.4 %divide_convert_fusion = bf16[8,1024,128]{2,1,0:T(8,128)(2,1)S(1)} fusion(f32[8,1024,128]{2,1,0:T(8,128)} %param.12, bf16[8,1024,128]{2,1,0:T(8,128)(2,1)} %param.13, f32[8,1024]{1,0:T(8,128)S(1)} %slice.66), kind=kLoop, calls=%fused_computation.1 | loop fusion | flops 4194304 | bytes 8421376 | tf_op jit(solution)/shard_map/convert_element_type | solution.py:88
  83.2 1.3 fusion
  84.5 1.2 copy.102
  85.7 3.7 %all-to-all-start.2 = ((bf16[16,8,32,128]{3,2,1,0:T(8,128)(2,1)}), bf16[16,8,32,128]{3,2,1,0:T(8,128)(2,1)S(1)}, u32[]{:S(2)}, u32[]{:S(2)}) async-start(bf16[16,8,32,128]{3,2,1,0:T(8,128)(2,1)} %copy.102), calls=%async_computation.2 | async-start | bytes 2097152 | tf_op jit(solution)/shard_map/all_to_all | solution.py:63
  89.4 1.0 copy.97
  90.4 2.3 %copy.103 = bf16[16,8,32,128]{3,2,1,0:T(8,128)(2,1)} copy(bf16[16,8,32,128]{3,2,0,1:T(8,128)(2,1)} %get-tuple-element.10) | data formatting | bytes 2097152 | tf_op jit(solution)/shard_map/split | solution.py:61
  92.7 15.5 %all-to-all-done.2 = bf16[16,8,32,128]{3,2,1,0:T(8,128)(2,1)S(1)} async-done(((bf16[16,8,32,128]{3,2,1,0:T(8,128)(2,1)}), bf16[16,8,32,128]{3,2,1,0:T(8,128)(2,1)S(1)}, u32[]{:S(2)}, u32[]{:S(2)}) %all-to-all-start.2) | async-done | bytes 1048608 | tf_op jit(solution)/shard_map/all_to_all | solution.py:63
  108.2 4.5 %all-to-all-start.3 = ((bf16[16,8,32,128]{3,2,1,0:T(8,128)(2,1)}), bf16[16,8,32,128]{3,2,1,0:T(8,128)(2,1)}, u32[]{:S(2)}, u32[]{:S(2)}) async-start(bf16[16,8,32,128]{3,2,1,0:T(8,128)(2,1)} %copy.103), calls=%async_computation.3 | async-start | bytes 2097152 | tf_op jit(solution)/shard_map/all_to_all | solution.py:63
  112.7 4.6 %divide_convert_fusion.2 = bf16[8,128,1024]{1,0,2:T(8,128)(2,1)} fusion(f32[8,128,1024]{1,0,2:T(8,128)} %copy.91, bf16[8,128,1024]{1,0,2:T(8,128)(2,1)} %copy.90, f32[8,1024]{0,1:T(8,128)} %copy.97), kind=kLoop, calls=%fused_computation.3 | loop fusion | flops 4194304 | bytes 8421376 | tf_op jit(solution)/shard_map/convert_element_type | solution.py:86
  117.2 1.0 copy.98
  118.3 4.1 %divide_convert_fusion.1 = bf16[8,128,1024]{1,0,2:T(8,128)(2,1)S(1)} fusion(f32[8,128,1024]{1,0,2:T(8,128)} %copy.94, bf16[8,128,1024]{1,0,2:T(8,128)(2,1)S(1)} %copy.93, f32[8,1024]{0,1:T(8,128)} %copy.98), kind=kLoop, calls=%fused_computation.2 | loop fusion | flops 4194304 | bytes 8421376 | tf_op jit(solution)/shard_map/convert_element_type | solution.py:87
  122.4 2.7 %pad_maximum_fusion = bf16[16,128,1024]{1,0,2:T(8,128)(2,1)} fusion(bf16[8,128,1024]{1,0,2:T(8,128)(2,1)S(1)} %divide_convert_fusion.1, bf16[8,128,1024]{1,0,2:T(8,128)(2,1)S(1)} %copy-done), kind=kLoop, calls=%fused_computation | loop fusion | flops 8388608 | bytes 8388608 | tf_op jit(solution)/shard_map/concatenate | solution.py:29
  125.1 3.6 %all-to-all-done.3 = bf16[16,8,32,128]{3,2,1,0:T(8,128)(2,1)} async-done(((bf16[16,8,32,128]{3,2,1,0:T(8,128)(2,1)}), bf16[16,8,32,128]{3,2,1,0:T(8,128)(2,1)}, u32[]{:S(2)}, u32[]{:S(2)}) %all-to-all-start.3) | async-done | bytes 1048608 | tf_op jit(solution)/shard_map/all_to_all | solution.py:63
  128.6 4.6 %all-to-all-start.1 = ((bf16[16,128,1024]{1,0,2:T(8,128)(2,1)}), bf16[16,128,1024]{1,0,2:T(8,128)(2,1)}, u32[]{:S(2)}, u32[]{:S(2)}) async-start(bf16[16,128,1024]{1,0,2:T(8,128)(2,1)} %pad_maximum_fusion), calls=%async_computation.1 | async-start | bytes 8388608 | tf_op jit(solution)/shard_map/all_to_all | solution.py:31
  135.2 2.9 %copy_bitcast_fusion = bf16[8,64,2048]{2,1,0:T(8,128)(2,1)} fusion(bf16[16,8,32,128]{3,2,1,0:T(8,128)(2,1)} %all-to-all-done.3, bf16[16,8,32,128]{3,2,1,0:T(8,128)(2,1)S(1)} %all-to-all-done.2), kind=kLoop, calls=%fused_computation.10 | loop fusion | flops 4194304 | bytes 4194304 | tf_op jit(solution)/shard_map/reshape | solution.py:54
  138.1 53.8 %all-to-all-done.1 = bf16[16,128,1024]{1,0,2:T(8,128)(2,1)} async-done(((bf16[16,128,1024]{1,0,2:T(8,128)(2,1)}), bf16[16,128,1024]{1,0,2:T(8,128)(2,1)}, u32[]{:S(2)}, u32[]{:S(2)}) %all-to-all-start.1) | async-done | bytes 4194336 | tf_op jit(solution)/shard_map/all_to_all | solution.py:31
  191.9 3.3 %copy.99 = bf16[16,128,1024]{1,2,0:T(8,128)(2,1)S(1)} copy(bf16[16,128,1024]{1,0,2:T(8,128)(2,1)} %all-to-all-done.1) | data formatting | bytes 8388608 | tf_op jit(solution)/shard_map/all_to_all | solution.py:31
  195.2 1.0 slice_bitcast_fusion
  196.1 1.9 copy.121
  198.0 1.9 copy.122
  (20 shorter events, 5.1 us)
Async XLA Ops:
  1.9 38.6 %all-to-all-start.4 = ((bf16[16,128,8]{1,2,0:T(8,128)(2,1)}), bf16[16,128,8]{1,2,0:T(8,128)(2,1)S(1)}, u32[]{:S(2)}, u32[]{:S(2)}) async-start(bf16[16,128,8]{1,2,0:T(8,128)(2,1)} %broadcast_in_dim.9), calls=%async_computation.4 | async-start | bytes 65536 | tf_op jit(solution)/shard_map/all_to_all | solution.py:9
  70.5 15.2 %all-to-all-start.5 = ((bf16[8,2048,8]{1,2,0:T(8,128)(2,1)}), bf16[8,2048,8]{1,2,0:T(8,128)(2,1)S(1)}, u32[]{:S(2)}, u32[]{:S(2)}) async-start(bf16[8,2048,8]{1,2,0:T(8,128)(2,1)} %broadcast_in_dim.11), calls=%async_computation.5 | async-start | bytes 524288 | tf_op jit(solution)/shard_map/all_to_all | solution.py:9
  85.7 22.5 %all-to-all-start.2 = ((bf16[16,8,32,128]{3,2,1,0:T(8,128)(2,1)}), bf16[16,8,32,128]{3,2,1,0:T(8,128)(2,1)S(1)}, u32[]{:S(2)}, u32[]{:S(2)}) async-start(bf16[16,8,32,128]{3,2,1,0:T(8,128)(2,1)} %copy.102), calls=%async_computation.2 | async-start | bytes 2097152 | tf_op jit(solution)/shard_map/all_to_all | solution.py:63
  108.2 20.5 %all-to-all-start.3 = ((bf16[16,8,32,128]{3,2,1,0:T(8,128)(2,1)}), bf16[16,8,32,128]{3,2,1,0:T(8,128)(2,1)}, u32[]{:S(2)}, u32[]{:S(2)}) async-start(bf16[16,8,32,128]{3,2,1,0:T(8,128)(2,1)} %copy.103), calls=%async_computation.3 | async-start | bytes 2097152 | tf_op jit(solution)/shard_map/all_to_all | solution.py:63
  118.2 4.1 %copy-start = (bf16[8,128,1024]{1,0,2:T(8,128)(2,1)S(1)}, bf16[8,128,1024]{1,0,2:T(8,128)(2,1)}, u32[]{:S(2)}) copy-start(bf16[8,128,1024]{1,0,2:T(8,128)(2,1)} %divide_convert_fusion.2) | copy-start | bytes 6291460
  128.6 63.2 %all-to-all-start.1 = ((bf16[16,128,1024]{1,0,2:T(8,128)(2,1)}), bf16[16,128,1024]{1,0,2:T(8,128)(2,1)}, u32[]{:S(2)}, u32[]{:S(2)}) async-start(bf16[16,128,1024]{1,0,2:T(8,128)(2,1)} %pad_maximum_fusion), calls=%async_computation.1 | async-start | bytes 8388608 | tf_op jit(solution)/shard_map/all_to_all | solution.py:31
where the time goes:
time: 203 us; the launch traced here: 201 us
  waiting for transfers between devices  72.8 us (36%)
  local copies, waits for them, and re-layouts  38.7 us (19%)
  other arithmetic  32.3 us (16%)
  starting transfers between devices  28 us (14%)
  blocking collectives  28 us (14%)
    all_to_all x1, waiting for transfers between devices, sent_together(): lax.all_to_all(both, axis, split_axis=split_dim, concat_axis=concat_dim,...  53.8 us
    all_to_all x1, blocking collectives, from_everyone(): lax.all_to_all(jnp.broadcast_to(array[None], (peers, *array.shape)), axis...  28 us
    unnamed x9, local copies, waits for them, and re-layouts  20 us
    all_to_all x2, waiting for transfers between devices, cut_exchange(): lax.all_to_all(piece, axis, split_axis=0, concat_axis=0, tiled=True)  19.1 us
    all_to_all x2, starting transfers between devices, from_everyone(): lax.all_to_all(jnp.broadcast_to(array[None], (peers, *array.shape)), axis...  15.2 us
    all_to_all x2, starting transfers between devices, cut_exchange(): lax.all_to_all(piece, axis, split_axis=0, concat_axis=0, tiled=True)  8.17 us
    split x3, local copies, waits for them, and re-layouts, cut_exchange(): jnp.split(tiles, piece_ends(tiles.shape[split_at], pieces), axis=split_at)  4.8 us
    all_to_all x1, starting transfers between devices, sent_together(): lax.all_to_all(both, axis, split_axis=split_dim, concat_axis=concat_dim,...  4.59 us
  transfers between devices with their start and end apart: 5, of which 3 were waited for; matrix products, arithmetic and copies ran while one was open for 29% of the time, Pallas kernels for 0%

commit v1 on v0

v1 whole, which is shorter than its diff:
```python
import functools
import math

import jax
import jax.numpy as jnp
from jax import lax
from jax.experimental import pallas as pl
from jax.experimental.pallas import tpu as pltpu
from jax.sharding import PartitionSpec as P

POWER = 17
GAIN = 2.0 ** (126 / POWER)
ROOT = 1.0 / (POWER * math.log(2.0))
LEAST = 1e-30
TAIL = 48
AHEAD = 3
F32, BF16 = jnp.float32, jnp.bfloat16


def encode(x, inverse):
    y = x * inverse
    power = y * y
    for _ in range(3):
        power = power * power
    return (power * y).astype(BF16)


def decode(code, factor):
    size = (jnp.exp2(jnp.log(jnp.abs(code).astype(F32)) * ROOT) * factor).astype(BF16)
    return jnp.where(code < 0, -size, size)


def in_parts(values):
    high = values.astype(BF16).astype(F32)
    rest = values - high
    middle = rest.astype(BF16).astype(F32)
    return high, middle, rest - middle


def for_peer(values, peer, width):
    at = peer * width // (2 * width) * 2 * width
    tile = values[:, at : at + 2 * width]
    rows = tile.shape[0] // 2
    low, high = tile[:rows], tile[rows:]
    left = lax.broadcasted_iota(jnp.int32, low.shape, 1) < width
    if peer % 2:
        return jnp.where(left, pltpu.roll(low, width, 1), high)
    return jnp.where(left, low, pltpu.roll(high, width, 1))


def send_kernel(peers, gate, d_gate, up, d_up, down, d_down, weight, gain, out, *scratch):
    (gate_in, d_gate_in, up_in, d_up_in, down_in, d_down_in) = scratch[:6]
    staged, most_gate, most_up, most_down, arrived, left = scratch[6:]
    experts, columns, lanes = down.shape
    width = columns // peers
    pairs = experts * width
    total = 3 * pairs

    def incoming(k, expert):
        source = (down, d_down, gate, d_gate, up, d_up)[k]
        target = (down_in, d_down_in, gate_in, d_gate_in, up_in, d_up_in)[k]
        return pltpu.make_async_copy(source.at[expert], target.at[expert], arrived.at[k, expert])

    def outgoing(k, first, rows, at):
        part = (slice(None), pl.ds(first, rows))
        return pltpu.make_async_copy(staged.at[part], out.at[part], left.at[k, at])

    for expert in range(AHEAD):
        for k in range(6):
            incoming(k, expert).start()

    lane = lax.broadcasted_iota(jnp.int32, most_down.shape, 1)

    def one(expert, carry):
        first = pl.multiple_of(expert * width, width)

        @pl.when(expert + AHEAD < experts)
        def _():
            for k in range(6):
                incoming(k, expert + AHEAD).start()

        incoming(0, expert).wait()
        incoming(1, expert).wait()
        x = down_in[expert] + d_down_in[expert].astype(F32)
        most = jnp.maximum(jnp.max(jnp.abs(x), axis=1, keepdims=True), LEAST)
        code = encode(x, GAIN / most)
        staged[:, pl.ds(first, width), :] = code.reshape(peers, width, lanes)
        most_down[...] = jnp.where(lane == expert, most, most_down[...])
        outgoing(0, first, width, expert).start()
        for k, (train, other, held) in enumerate(
            ((gate_in, d_gate_in, most_gate), (up_in, d_up_in, most_up))
        ):
            incoming(2 + 2 * k, expert).wait()
            incoming(3 + 2 * k, expert).wait()
            x = train[expert] + other[expert].astype(F32)
            most = jnp.maximum(jnp.max(jnp.abs(x), axis=0, keepdims=True), LEAST)
            code = encode(x, GAIN / most).T
            at = pl.multiple_of(pairs + expert * 2 * width + k * width, width)
            staged[:, pl.ds(at, width), :] = code.reshape(peers, width, lanes)
            held[pl.ds(expert, 1), :] = most
        outgoing(1, pl.multiple_of(pairs + expert * 2 * width, width), 2 * width, expert).start()
        return carry

    lax.fori_loop(0, experts, one, 0)
    parts = tuple(
        zip(*(in_parts(v) for v in (most_down[...].T[:8], most_gate[...], most_up[...])))
    )
    router = weight[...] * gain[...]
    for peer in range(peers):
        rows = [for_peer(part, peer, width) for split in parts for part in split]
        rows = jnp.concatenate([*rows, jnp.zeros_like(rows[0]), router], axis=0)
        staged[peer, total:, :] = rows.astype(BF16)
    outgoing(0, total, TAIL, experts).start()
    for expert in range(experts):
        outgoing(0, expert * width, width, expert).wait()
        outgoing(1, pairs + expert * 2 * width, 2 * width, expert).wait()
    outgoing(0, total, TAIL, experts).wait()


def factors(parts, table, scale):
    peers, rows, lanes = parts.shape
    half = lanes // 2
    for row in range(rows):
        local = parts[:, row, :]
        most = jnp.max(local, axis=0, keepdims=True)
        scale[row : row + 1, :] = most[:, :half]
        scale[row + rows : row + rows + 1, :] = pltpu.roll(most, half, 1)[:, :half]
        factor = local * ((1.0 / GAIN) / most)
        factor = jnp.concatenate([factor, jnp.zeros((lanes - peers, lanes), F32)], axis=0)
        table[row] = factor.T


def spread(codes, expert, first, width, table, out):
    rows = table.shape[0]
    half = pl.multiple_of(lax.div(expert, rows) * width, width)
    factor = table[lax.rem(expert, rows), pl.ds(half, width), :]
    for peer in range(codes.shape[1]):
        got = codes[expert, peer, first : first + width, :]
        out[expert, :, peer * 128 : (peer + 1) * 128] = decode(got, factor[:, peer : peer + 1])


def take_kernel(first, count, got, *refs):
    outs, scales = refs[:count], refs[count : 2 * count]
    extra = refs[2 * count : -(2 * count + 5)]
    codes, tail = refs[-(2 * count + 5) : -(2 * count + 3)]
    tables, staged = refs[-(2 * count + 3) : -(count + 3)], refs[-(count + 3) : -3]
    arrived, left, tailed = refs[-3:]
    experts, peers, rows, lanes = codes.shape
    width = rows // count

    def incoming(expert):
        start = expert * rows + first
        return pltpu.make_async_copy(
            got.at[:, pl.ds(start, rows)], codes.at[expert], arrived.at[expert]
        )

    def outgoing(k, expert):
        return pltpu.make_async_copy(staged[k].at[expert], outs[k].at[expert], left.at[k, expert])

    last = pltpu.make_async_copy(got.at[:, pl.ds(3 * experts * width, TAIL)], tail, tailed)
    last.start()
    for expert in range(AHEAD):
        incoming(expert).start()
    last.wait()
    ends = tail[...].astype(F32)
    for k in range(count):
        at = 4 * (k + (count > 1))
        local = ends[:, at : at + 4] + ends[:, at + 12 : at + 16] + ends[:, at + 24 : at + 28]
        factors(local, tables[k], scales[k])
    for router in extra:
        for peer in range(peers):
            row = ends[peer, TAIL - 8 :].astype(BF16)
            for owner in range(router.shape[0]):
                router[owner, :, peer * lanes : (peer + 1) * lanes] = row

    def one(expert, carry):
        @pl.when(expert + AHEAD < experts)
        def _():
            incoming(expert + AHEAD).start()

        incoming(expert).wait()
        for k in range(count):
            spread(codes, expert, k * width, width, tables[k], staged[k])
            outgoing(k, expert).start()
        return carry

    lax.fori_loop(0, experts, one, 0)
    for expert in range(experts):
        for k in range(count):
            outgoing(k, expert).wait()


def cost(elements, operations):
    return pl.CostEstimate(flops=elements * operations, bytes_accessed=elements * 8, transcendentals=0)


ANY = pl.BlockSpec(memory_space=pl.ANY)
WHOLE = pl.BlockSpec(memory_space=pltpu.VMEM)
DMA = pltpu.SemaphoreType.DMA


def send(arrays, weight, gain, peers):
    experts, columns, lanes = arrays[4].shape
    rows = 3 * experts * columns // peers + TAIL
    return pl.pallas_call(
        functools.partial(send_kernel, peers),
        in_specs=[ANY] * 6 + [WHOLE] * 2,
        out_specs=ANY,
        out_shape=jax.ShapeDtypeStruct((peers, rows, lanes), BF16),
        scratch_shapes=[
            *(pltpu.VMEM(a.shape, a.dtype) for a in arrays),
            pltpu.VMEM((peers, rows, lanes), BF16),
            pltpu.VMEM((experts, columns), F32),
            pltpu.VMEM((experts, columns), F32),
            pltpu.VMEM((columns, lanes), F32),
            DMA((6, experts)),
            DMA((2, experts + 1)),
        ],
        cost_estimate=cost(3 * arrays[4].size, 20),
        name="send",
    )(*arrays, weight, gain)


def take(got, first, count, owners, experts, width):
    peers, _, lanes = got.shape
    out = jax.ShapeDtypeStruct((experts, width, peers * lanes), BF16)
    scale = jax.ShapeDtypeStruct((experts, width), F32)
    router = [jax.ShapeDtypeStruct((owners, 8, peers * lanes), BF16)] if owners else []
    return pl.pallas_call(
        functools.partial(take_kernel, first, count),
        in_specs=[ANY],
        out_specs=[ANY] * count + [WHOLE] * (count + len(router)),
        out_shape=[out] * count + [scale] * count + router,
        scratch_shapes=[
            pltpu.VMEM((experts, peers, count * width, lanes), BF16),
            pltpu.VMEM((peers, TAIL, lanes), BF16),
            *[pltpu.VMEM((4, lanes, lanes), F32)] * count,
            *[pltpu.VMEM((experts, width, peers * lanes), BF16)] * count,
            DMA((experts,)),
            DMA((count, experts)),
            DMA(()),
        ],
        cost_estimate=cost(count * experts * width * peers * lanes, 20),
        name="take_pair" if count > 1 else "take_down",
    )(got)


def exchange(array, axis):
    return lax.all_to_all(array, axis, 0, 0, tiled=True)


def shards(
    train_gate, other_gate, train_up, other_up, train_down, other_down, router_weight, router_gain
):
    peers, owners = lax.axis_size("rows"), lax.axis_size("owner")
    experts, columns, _ = train_down.shape
    width = columns // peers
    arrays = (train_gate, other_gate, train_up, other_up, train_down, other_down)
    got = exchange(send(arrays, router_weight.T, router_gain[None, :], peers), "rows")
    ready_down, scale_down, router = take(got, 0, 1, owners, experts, width)
    router = exchange(router, "owner")
    gate, up, scale_gate, scale_up = take(got, experts * width, 2, 0, experts, width)
    serve_router = router.reshape(-1, router.shape[2]).T
    ready_gate, ready_up = jnp.swapaxes(gate, 1, 2), jnp.swapaxes(up, 1, 2)
    return (ready_gate, ready_up, ready_down, scale_gate, scale_up, scale_down, serve_router)


def solution(mesh):
    placed = (
        P("owner", "rows", None),
        P("owner", "rows", None),
        P("owner", "rows", None),
        P("owner", "rows", None),
        P("owner", None, "rows"),
        P("owner", None, "rows"),
        P("rows", "owner"),
        P("rows"),
    )
    return jax.shard_map(
        shards,
        mesh=mesh,
        in_specs=placed,
        out_specs=(
            P("owner", None, "rows"),
            P("owner", None, "rows"),
            P("owner", "rows", None),
            P("owner", "rows"),
            P("owner", "rows"),
            P("owner", "rows"),
            P(),
        ),
        check_vma=False,
    )
```

time: 203 us -> 114 us (0.56)
  waiting for transfers between devices: 72.8 us -> 0.01 us
  blocking collectives: 28 us -> 83.2 us
  local copies, waits for them, and re-layouts: 38.7 us -> 0.71 us
  other arithmetic: 32.3 us -> 0 us
  Pallas kernels: 0 us -> 22.8 us
  starting transfers between devices: 28 us -> 6.25 us
    all_to_all x5 -> x1, waiting for transfers between devices: 72.8 us -> 0.01 us  [exchange(): return lax.all_to_all(array, axis, 0, 0, tiled=True)]
    all_to_all x1, blocking collectives: 28 us -> 83.2 us  [exchange(): return lax.all_to_all(array, axis, 0, 0, tiled=True)]
    pallas_call x0 -> x3, Pallas kernels: none -> 22.8 us  [the longest x2 12.1 us: take(): pl.pallas_call(functools.partial(take_kernel, first, count), in_specs=[AN...]
    all_to_all x5 -> x1, starting transfers between devices: 28 us -> 6.25 us  [exchange(): return lax.all_to_all(array, axis, 0, 0, tiled=True)]
    unnamed x9 -> x1, local copies, waits for them, and re-layouts: 20 us -> 0.71 us
    reduce_max x4 -> x0, other arithmetic: 13.9 us -> none  [the longest x1 4.05 us: shards(): jnp.max(jnp.abs(latest_gate), axis=1)]
    convert_element_type x4 -> x0, other arithmetic: 12.8 us -> none  [the longest x1 4.56 us: shards(): (latest_gate / jnp.expand_dims(scale_gate, 1)).astype(jnp.bfloat16)]
    slice x8 -> x0, local copies, waits for them, and re-layouts: 5.82 us -> none  [the longest x2 3.79 us: sent_together(): lax.slice_in_dim(filled, at, at + a.shape[along], axis=along)]
  transfers between devices with their start and end apart: 5 -> 1, of which waited for: 3 -> 0; matrix products, arithmetic and copies ran while one was open for 29% -> 0% of each run, Pallas kernels for 0% -> 6%
where the time goes in v1:
time: 114 us
  blocking collectives  83.2 us (73%)
  Pallas kernels  22.8 us (20%)
  starting transfers between devices  6.25 us (5%)
    all_to_all x1, blocking collectives, exchange(): return lax.all_to_all(array, axis, 0, 0, tiled=True)  83.2 us
    pallas_call x2, Pallas kernels, take(): pl.pallas_call(functools.partial(take_kernel, first, count), in_specs=[AN...  12.1 us
    pallas_call x1, Pallas kernels, send(): pl.pallas_call(functools.partial(send_kernel, peers), in_specs=[ANY] * 6...  10.7 us
    all_to_all x1, starting transfers between devices, exchange(): return lax.all_to_all(array, axis, 0, 0, tiled=True)  6.25 us
  transfers between devices with their start and end apart: 1, of which 0 were waited for; matrix products, arithmetic and copies ran while one was open for 0% of the time, Pallas kernels for 6%

profile of v1, /device:TPU:1, one launch (start us, length us, event | category | flops | bytes accessed | tf_op | source)
XLA Modules:
  0.0 113.6 jit_solution(2189474176137871834)
XLA Ops:
  0.6 10.7 %send.1 = bf16[16,1584,128]{2,1,0:T(8,128)(2,1)} custom-call(f32[8,128,1024]{2,1,0:T(8,128)} %gate.1, bf16[8,128,1024]{2,1,0:T(8,128)(2,1)} %d_gate.1, f32[8,128,1024]{2,1,0:T(8,128)} %up.1, bf16[8,128,1024]{2,1,0:T(8,128)(2,1)} %d_up.1, f32[8,1024,128]{2,1,0:T(8,128)} %down.1, bf16[8,1024,128]{2,1,0:T(8,128)(2,1)} %d_down.1, f32[8,128]{1,0:T(8,128)} %bitcast.8, ...), custom_call_target="tpu_custom_call" | custom-call | flops 62914560 | bytes 25165824 | tf_op jit(solution)/shard_map/send/pallas_call | solution.py:205
  11.4 83.2 %all_to_all.10.got = bf16[16,1584,128]{2,1,0:T(8,128)(2,1)} all-to-all(bf16[16,1584,128]{2,1,0:T(8,128)(2,1)} %send.1), channel_id=1, replica_groups=mesh['owner'=8,'rows'=16] {'rows'}, dimensions={0} | all-to-all | bytes 12976128 | tf_op jit(solution)/shard_map/all_to_all | solution.py:249
  94.5 5.4 %take_down.1 = (bf16[8,64,2048]{2,1,0:T(8,128)(2,1)}, f32[8,64]{1,0:T(8,128)}, bf16[8,8,2048]{2,1,0:T(8,128)(2,1)}) custom-call(bf16[16,1584,128]{2,1,0:T(8,128)(2,1)} %all_to_all.10.got), custom_call_target="tpu_custom_call" | custom-call | flops 20971520 | bytes 8388608 | tf_op jit(solution)/shard_map/take_down/pallas_call | solution.py:229
  99.9 6.2 %all-to-all-start.1 = ((bf16[8,8,2048]{2,1,0:T(8,128)(2,1)}), bf16[8,8,2048]{2,1,0:T(8,128)(2,1)S(1)}, u32[]{:S(2)}, u32[]{:S(2)}) async-start(bf16[8,8,2048]{2,1,0:T(8,128)(2,1)} %get-tuple-element.20), calls=%async_computation.1 | async-start | bytes 524288 | tf_op jit(solution)/shard_map/all_to_all | solution.py:249
  106.1 6.7 %take_pair.1 = (bf16[8,64,2048]{2,1,0:T(8,128)(2,1)}, bf16[8,64,2048]{2,1,0:T(8,128)(2,1)}, f32[8,64]{1,0:T(8,128)}, f32[8,64]{1,0:T(8,128)}) custom-call(bf16[16,1584,128]{2,1,0:T(8,128)(2,1)} %all_to_all.10.got), custom_call_target="tpu_custom_call" | custom-call | flops 41943040 | bytes 16777216 | tf_op jit(solution)/shard_map/take_pair/pallas_call | solution.py:229
  112.9 0.0 all-to-all-done.1
  112.9 0.7 copy.16
Async XLA Ops:
  99.9 13.0 %all-to-all-start.1 = ((bf16[8,8,2048]{2,1,0:T(8,128)(2,1)}), bf16[8,8,2048]{2,1,0:T(8,128)(2,1)S(1)}, u32[]{:S(2)}, u32[]{:S(2)}) async-start(bf16[8,8,2048]{2,1,0:T(8,128)(2,1)} %get-tuple-element.20), calls=%async_computation.1 | async-start | bytes 524288 | tf_op jit(solution)/shard_map/all_to_all | solution.py:249

commit v2 on v1

v2 whole, which is shorter than its diff:
```python
import functools
import math

import jax
import jax.numpy as jnp
from jax import lax
from jax.experimental import pallas as pl
from jax.experimental.pallas import tpu as pltpu
from jax.sharding import PartitionSpec as P

POWER = 17
GAIN = 2.0 ** (126 / POWER)
ROOT = (1.0 / POWER - 1.0) / math.log(2.0)
TINY = 2.0**-126
LEAST = 1e-30
TAIL = 48
AHEAD = 2
F32, BF16 = jnp.float32, jnp.bfloat16


def encode(x, inverse):
    y = x * inverse
    power = y * y
    for _ in range(3):
        power = power * power
    return (power * y).astype(BF16)


def decode(code, factor):
    code = code.astype(F32)
    size = jnp.maximum(jnp.abs(code), TINY)
    return (jnp.exp2(jnp.log(size) * ROOT) * code * factor).astype(BF16)


def in_parts(values):
    high = values.astype(BF16).astype(F32)
    rest = values - high
    middle = rest.astype(BF16).astype(F32)
    return high, middle, rest - middle


def for_peer(values, peer, width):
    at = peer * width // (2 * width) * 2 * width
    tile = values[:, at : at + 2 * width]
    rows = tile.shape[0] // 2
    low, high = tile[:rows], tile[rows:]
    left = lax.broadcasted_iota(jnp.int32, low.shape, 1) < width
    if peer % 2:
        return jnp.where(left, pltpu.roll(low, width, 1), high)
    return jnp.where(left, low, pltpu.roll(high, width, 1))


def send_kernel(peers, gate, d_gate, up, d_up, down, d_down, weight, gain, out, *scratch):
    (gate_in, d_gate_in, up_in, d_up_in, down_in, d_down_in) = scratch[:6]
    most_gate, most_up, most_down, weight_in, gain_in, arrived, small = scratch[6:]
    experts, columns, lanes = down.shape
    width = columns // peers
    pairs = experts * width
    total = 3 * pairs

    def incoming(k, expert):
        source = (down, d_down, gate, d_gate, up, d_up)[k]
        target = (down_in, d_down_in, gate_in, d_gate_in, up_in, d_up_in)[k]
        return pltpu.make_async_copy(source.at[expert], target.at[expert], arrived.at[k, expert])

    for expert in range(AHEAD):
        for k in range(6):
            incoming(k, expert).start()
    load_weight = pltpu.make_async_copy(weight, weight_in, small.at[0])
    load_gain = pltpu.make_async_copy(gain, gain_in, small.at[1])
    load_weight.start()
    load_gain.start()
    lane = lax.broadcasted_iota(jnp.int32, (width, lanes), 1)
    row = lax.broadcasted_iota(jnp.int32, (experts, lanes), 0)

    def one(expert, carry):
        first = pl.multiple_of(expert * width, width)

        @pl.when(expert + AHEAD < experts)
        def _():
            for k in range(6):
                incoming(k, expert + AHEAD).start()

        incoming(0, expert).wait()
        incoming(1, expert).wait()
        for peer in range(peers):
            part = slice(peer * width, (peer + 1) * width)
            x = down_in[expert, part, :] + d_down_in[expert, part, :].astype(F32)
            most = jnp.maximum(jnp.max(jnp.abs(x), axis=1, keepdims=True), LEAST)
            out[peer, pl.ds(first, width), :] = encode(x, GAIN / most)
            most_down[part, :] = jnp.where(lane == expert, most, most_down[part, :])
        for k, (train, other, held) in enumerate(
            ((gate_in, d_gate_in, most_gate), (up_in, d_up_in, most_up))
        ):
            incoming(2 + 2 * k, expert).wait()
            incoming(3 + 2 * k, expert).wait()
            at = pl.multiple_of(pairs + expert * 2 * width + k * width, width)
            for pair in range(peers // 2):
                part = slice(pair * lanes, (pair + 1) * lanes)
                x = train[expert, :, part] + other[expert, :, part].astype(F32)
                most = jnp.maximum(jnp.max(jnp.abs(x), axis=0, keepdims=True), LEAST)
                code = encode(x, GAIN / most).T
                out[2 * pair, pl.ds(at, width), :] = code[:width]
                out[2 * pair + 1, pl.ds(at, width), :] = code[width:]
                held[:, part] = jnp.where(row == expert, most, held[:, part])
        return carry

    lax.fori_loop(0, experts, one, 0)
    parts = tuple(
        zip(*(in_parts(v) for v in (most_down[...].T[:8], most_gate[...], most_up[...])))
    )
    load_weight.wait()
    load_gain.wait()
    router = weight_in[...] * gain_in[...]
    for peer in range(peers):
        rows = [for_peer(part, peer, width) for split in parts for part in split]
        rows = jnp.concatenate([*rows, jnp.zeros_like(rows[0]), router], axis=0)
        out[peer, total:, :] = rows.astype(BF16)


def factors(parts, table, scale):
    peers, rows, lanes = parts.shape
    half = lanes // 2
    for row in range(rows):
        local = parts[:, row, :]
        most = jnp.max(local, axis=0, keepdims=True)
        scale[row : row + 1, :] = most[:, :half]
        scale[row + rows : row + rows + 1, :] = pltpu.roll(most, half, 1)[:, :half]
        factor = local * ((1.0 / GAIN) / most)
        factor = jnp.concatenate([factor, jnp.zeros((lanes - peers, lanes), F32)], axis=0)
        table[row] = factor.T


def copies_kernel(tile, router):
    lanes = tile.shape[2]
    for peer in range(tile.shape[0]):
        for owner in range(router.shape[0]):
            router[owner, :, peer * lanes : (peer + 1) * lanes] = tile[peer]


def take_kernel(got, *refs):
    outs, scales, codes, tail = refs[:3], refs[3:6], refs[6], refs[7]
    tables, staged, scaled = refs[8:11], refs[11:14], refs[14:17]
    arrived, left, tailed, scaling = refs[17:]
    experts, peers, rows, lanes = codes.shape
    width = rows // 3

    def incoming(k, expert):
        start = expert * width if k == 0 else (experts + 2 * expert) * width
        size, to = (width, 0) if k == 0 else (2 * width, width)
        return pltpu.make_async_copy(
            got.at[:, pl.ds(pl.multiple_of(start, width), size)],
            codes.at[expert, :, pl.ds(to, size)],
            arrived.at[k, expert],
        )

    def outgoing(k, expert):
        return pltpu.make_async_copy(staged[k].at[expert], outs[k].at[expert], left.at[k, expert])

    last = pltpu.make_async_copy(got.at[:, pl.ds(experts * rows, TAIL)], tail, tailed)
    last.start()
    for expert in range(AHEAD):
        incoming(0, expert).start()
        incoming(1, expert).start()
    last.wait()
    ends = tail[...].astype(F32)
    for k in range(3):
        at = 4 * k
        local = ends[:, at : at + 4] + ends[:, at + 12 : at + 16] + ends[:, at + 24 : at + 28]
        factors(local, tables[k], scaled[k])
    scalings = [pltpu.make_async_copy(scaled[k], scales[k], scaling.at[k]) for k in range(3)]
    for copy in scalings:
        copy.start()

    def one(expert, carry):
        @pl.when(expert + AHEAD < experts)
        def _():
            incoming(0, expert + AHEAD).start()
            incoming(1, expert + AHEAD).start()

        half = pl.multiple_of(lax.div(expert, 4) * width, width)
        for k in range(3):
            if k < 2:
                incoming(k, expert).wait()
            factor = tables[k][lax.rem(expert, 4), pl.ds(half, width), :]
            for peer in range(peers):
                code = codes[expert, peer, k * width : (k + 1) * width, :]
                staged[k][expert, :, peer * lanes : (peer + 1) * lanes] = decode(
                    code, factor[:, peer : peer + 1]
                )
            outgoing(k, expert).start()
        return carry

    lax.fori_loop(0, experts, one, 0)
    for expert in range(experts):
        for k in range(3):
            outgoing(k, expert).wait()
    for copy in scalings:
        copy.wait()


def cost(elements, operations):
    return pl.CostEstimate(flops=elements * operations, bytes_accessed=elements * 8, transcendentals=0)


HBM = pl.BlockSpec(memory_space=pltpu.HBM)
WHOLE = pl.BlockSpec(memory_space=pltpu.VMEM)
DMA = pltpu.SemaphoreType.DMA


def in_hbm(array):
    return pltpu.with_memory_space_constraint(array, pltpu.HBM)


def send(arrays, weight, gain, peers):
    experts, columns, lanes = arrays[4].shape
    rows = 3 * experts * columns // peers + TAIL
    return pl.pallas_call(
        functools.partial(send_kernel, peers),
        in_specs=[HBM] * 8,
        out_specs=WHOLE,
        out_shape=pltpu.VMEM((peers, rows, lanes), BF16),
        scratch_shapes=[
            *(pltpu.VMEM(a.shape, a.dtype) for a in arrays),
            pltpu.VMEM((experts, columns), F32),
            pltpu.VMEM((experts, columns), F32),
            pltpu.VMEM((columns, lanes), F32),
            pltpu.VMEM(weight.shape, F32),
            pltpu.VMEM(gain.shape, F32),
            DMA((6, experts)),
            DMA((2,)),
        ],
        compiler_params=pltpu.CompilerParams(vmem_limit_bytes=32 << 20),
        cost_estimate=cost(3 * arrays[4].size, 20),
        name="send",
    )(*(in_hbm(a) for a in (*arrays, weight, gain)))


def copies(got, owners):
    peers, rows, lanes = got.shape
    return pl.pallas_call(
        copies_kernel,
        grid=(1,),
        in_specs=[pl.BlockSpec((peers, 8, lanes), lambda i: (0, rows // 8 - 1, 0))],
        out_specs=WHOLE,
        out_shape=jax.ShapeDtypeStruct((owners, 8, peers * lanes), BF16),
        name="copies",
    )(in_hbm(got))


def take(got, experts, width):
    peers, _, lanes = got.shape
    shape = (experts, width, peers * lanes)
    return pl.pallas_call(
        take_kernel,
        in_specs=[HBM],
        out_specs=[HBM] * 6,
        out_shape=[jax.ShapeDtypeStruct(shape, BF16)] * 3
        + [jax.ShapeDtypeStruct((experts, width), F32)] * 3,
        scratch_shapes=[
            pltpu.VMEM((experts, peers, 3 * width, lanes), BF16),
            pltpu.VMEM((peers, TAIL, lanes), BF16),
            *[pltpu.VMEM((4, lanes, lanes), F32)] * 3,
            *[pltpu.VMEM(shape, BF16)] * 3,
            *[pltpu.VMEM((experts, width), F32)] * 3,
            DMA((2, experts)),
            DMA((3, experts)),
            DMA(()),
            DMA((3,)),
        ],
        compiler_params=pltpu.CompilerParams(vmem_limit_bytes=58 << 20),
        cost_estimate=cost(3 * experts * width * peers * lanes, 20),
        name="take",
    )(in_hbm(got))


def exchange(array, axis):
    return lax.all_to_all(array, axis, 0, 0, tiled=True)


def shards(
    train_gate, other_gate, train_up, other_up, train_down, other_down, router_weight, router_gain
):
    peers, owners = lax.axis_size("rows"), lax.axis_size("owner")
    experts, columns, _ = train_down.shape
    width = columns // peers
    arrays = (train_gate, other_gate, train_up, other_up, train_down, other_down)
    got = exchange(send(arrays, router_weight.T, router_gain[None, :], peers), "rows")
    router = exchange(copies(got, owners), "owner")
    ready_down, gate, up, scale_down, scale_gate, scale_up = take(got, experts, width)
    serve_router = router.reshape(-1, router.shape[2]).T
    ready_gate, ready_up = jnp.swapaxes(gate, 1, 2), jnp.swapaxes(up, 1, 2)
    return (ready_gate, ready_up, ready_down, scale_gate, scale_up, scale_down, serve_router)


def solution(mesh):
    placed = (
        P("owner", "rows", None),
        P("owner", "rows", None),
        P("owner", "rows", None),
        P("owner", "rows", None),
        P("owner", None, "rows"),
        P("owner", None, "rows"),
        P("rows", "owner"),
        P("rows"),
    )
    return jax.shard_map(
        shards,
        mesh=mesh,
        in_specs=placed,
        out_specs=(
            P("owner", None, "rows"),
            P("owner", None, "rows"),
            P("owner", "rows", None),
            P("owner", "rows"),
            P("owner", "rows"),
            P("owner", "rows"),
            P(),
        ),
        check_vma=False,
    )
```

time: 114 us -> 108 us (0.947)
  Pallas kernels: 22.8 us -> 17.4 us
    pallas_call x3, Pallas kernels: 22.8 us -> 17.4 us  [the longest x1 8.17 us: send(): pl.pallas_call(functools.partial(send_kernel, peers), in_specs=[HBM] * 8,...]
  transfers between devices with their start and end apart: 1 -> 1, of which waited for: 0 -> 0; matrix products, arithmetic and copies ran while one was open for 0% -> 0% of each run, Pallas kernels for 6% -> 7%
where the time goes in v2:
time: 108 us
  blocking collectives  82.9 us (77%)
  Pallas kernels  17.4 us (16%)
  starting transfers between devices  6.24 us (6%)
    all_to_all x1, blocking collectives, exchange(): return lax.all_to_all(array, axis, 0, 0, tiled=True)  82.9 us
    pallas_call x1, Pallas kernels, send(): pl.pallas_call(functools.partial(send_kernel, peers), in_specs=[HBM] * 8,...  8.17 us
    pallas_call x1, Pallas kernels, take(): pl.pallas_call(take_kernel, in_specs=[HBM], out_specs=[HBM] * 6, out_shap...  7.75 us
    all_to_all x1, starting transfers between devices, exchange(): return lax.all_to_all(array, axis, 0, 0, tiled=True)  6.24 us
  transfers between devices with their start and end apart: 1, of which 0 were waited for; matrix products, arithmetic and copies ran while one was open for 0% of the time, Pallas kernels for 7%

profile of v2, /device:TPU:1, one launch (start us, length us, event | category | flops | bytes accessed | tf_op | source)
XLA Modules:
  0.0 108.0 jit_solution(4367210378469538710)
XLA Ops:
  0.6 8.2 %send.1 = bf16[16,1584,128]{2,1,0:T(8,128)(2,1)S(1)} custom-call(f32[8,128,1024]{2,1,0:T(8,128)} %gate.1, bf16[8,128,1024]{2,1,0:T(8,128)(2,1)} %d_gate.1, f32[8,128,1024]{2,1,0:T(8,128)} %up.1, bf16[8,128,1024]{2,1,0:T(8,128)(2,1)} %d_up.1, f32[8,1024,128]{2,1,0:T(8,128)} %down.1, bf16[8,1024,128]{2,1,0:T(8,128)(2,1)} %d_down.1, f32[8,128]{1,0:T(8,128)} %bitcast.8, ...), custom_call_target="tpu_custom_call" | custom-call | flops 62914560 | bytes 25165824 | tf_op jit(solution)/shard_map/send/pallas_call | solution.py:218
  8.8 82.9 %all_to_all.10.got.tile = bf16[16,1584,128]{2,1,0:T(8,128)(2,1)} all-to-all(bf16[16,1584,128]{2,1,0:T(8,128)(2,1)S(1)} %send.1), channel_id=1, replica_groups=mesh['owner'=8,'rows'=16] {'rows'}, dimensions={0} | all-to-all | bytes 12976128 | tf_op jit(solution)/shard_map/all_to_all | solution.py:278
  91.8 1.5 %copies.1 = bf16[8,8,2048]{2,1,0:T(8,128)(2,1)} custom-call(bf16[16,1584,128]{2,1,0:T(8,128)(2,1)} %all_to_all.10.got.tile), custom_call_target="tpu_custom_call" | custom-call | tf_op jit(solution)/shard_map/copies/pallas_call | solution.py:241
  93.2 6.2 %all-to-all-start.1 = ((bf16[8,8,2048]{2,1,0:T(8,128)(2,1)}), bf16[8,8,2048]{2,1,0:T(8,128)(2,1)S(1)}, u32[]{:S(2)}, u32[]{:S(2)}) async-start(bf16[8,8,2048]{2,1,0:T(8,128)(2,1)} %copies.1), calls=%async_computation.1 | async-start | bytes 524288 | tf_op jit(solution)/shard_map/all_to_all | solution.py:278
  99.5 7.7 %take.1 = (bf16[8,64,2048]{2,1,0:T(8,128)(2,1)}, bf16[8,64,2048]{2,1,0:T(8,128)(2,1)}, bf16[8,64,2048]{2,1,0:T(8,128)(2,1)}, f32[8,64]{1,0:T(8,128)}, f32[8,64]{1,0:T(8,128)}, /*index=5*/f32[8,64]{1,0:T(8,128)}) custom-call(bf16[16,1584,128]{2,1,0:T(8,128)(2,1)} %all_to_all.10.got.tile), custom_call_target="tpu_custom_call" | custom-call | flops 62914560 | bytes 25165824 | tf_op jit(solution)/shard_map/take/pallas_call | solution.py:254
  107.2 0.0 all-to-all-done.1
  107.2 0.7 copy.16
Async XLA Ops:
  93.2 14.0 %all-to-all-start.1 = ((bf16[8,8,2048]{2,1,0:T(8,128)(2,1)}), bf16[8,8,2048]{2,1,0:T(8,128)(2,1)S(1)}, u32[]{:S(2)}, u32[]{:S(2)}) async-start(bf16[8,8,2048]{2,1,0:T(8,128)(2,1)} %copies.1), calls=%async_computation.1 | async-start | bytes 524288 | tf_op jit(solution)/shard_map/all_to_all | solution.py:278

commit v3 on v2

--- a/solution.py
+++ b/solution.py
@@ -13,7 +13,7 @@
 ROOT = (1.0 / POWER - 1.0) / math.log(2.0)
 TINY = 2.0**-126
 LEAST = 1e-30
-TAIL = 48
+TAIL = 32
 AHEAD = 2
 F32, BF16 = jnp.float32, jnp.bfloat16
 
@@ -35,8 +35,7 @@
 def in_parts(values):
     high = values.astype(BF16).astype(F32)
     rest = values - high
-    middle = rest.astype(BF16).astype(F32)
-    return high, middle, rest - middle
+    return high, rest.astype(BF16).astype(F32)
 
 
 def for_peer(values, peer, width):
@@ -114,7 +113,7 @@
     router = weight_in[...] * gain_in[...]
     for peer in range(peers):
         rows = [for_peer(part, peer, width) for split in parts for part in split]
-        rows = jnp.concatenate([*rows, jnp.zeros_like(rows[0]), router], axis=0)
+        rows = jnp.concatenate([*rows, router], axis=0)
         out[peer, total:, :] = rows.astype(BF16)
 
 
@@ -166,7 +165,7 @@
     ends = tail[...].astype(F32)
     for k in range(3):
         at = 4 * k
-        local = ends[:, at : at + 4] + ends[:, at + 12 : at + 16] + ends[:, at + 24 : at + 28]
+        local = ends[:, at : at + 4] + ends[:, at + 12 : at + 16]
         factors(local, tables[k], scaled[k])
     scalings = [pltpu.make_async_copy(scaled[k], scales[k], scaling.at[k]) for k in range(3)]
     for copy in scalings:

time: 108 us -> 108 us (level)
  no operation moved by 1% of the time
where the time goes in v3:
time: 108 us; the launch traced here: 107 us
  blocking collectives  82 us (76%)
  Pallas kernels  17.4 us (16%)
  starting transfers between devices  6.5 us (6%)
    all_to_all x1, blocking collectives, exchange(): return lax.all_to_all(array, axis, 0, 0, tiled=True)  82 us
    pallas_call x1, Pallas kernels, send(): pl.pallas_call(functools.partial(send_kernel, peers), in_specs=[HBM] * 8,...  8.14 us
    pallas_call x1, Pallas kernels, take(): pl.pallas_call(take_kernel, in_specs=[HBM], out_specs=[HBM] * 6, out_shap...  7.72 us
    all_to_all x1, starting transfers between devices, exchange(): return lax.all_to_all(array, axis, 0, 0, tiled=True)  6.5 us
  transfers between devices with their start and end apart: 1, of which 0 were waited for; matrix products, arithmetic and copies ran while one was open for 0% of the time, Pallas kernels for 7%

profile of v3, /device:TPU:1, one launch (start us, length us, event | category | flops | bytes accessed | tf_op | source)
XLA Modules:
  0.0 107.2 jit_solution(2876914256270491785)
XLA Ops:
  0.6 8.1 %send.1 = bf16[16,1568,128]{2,1,0:T(8,128)(2,1)S(1)} custom-call(f32[8,128,1024]{2,1,0:T(8,128)} %gate.1, bf16[8,128,1024]{2,1,0:T(8,128)(2,1)} %d_gate.1, f32[8,128,1024]{2,1,0:T(8,128)} %up.1, bf16[8,128,1024]{2,1,0:T(8,128)(2,1)} %d_up.1, f32[8,1024,128]{2,1,0:T(8,128)} %down.1, bf16[8,1024,128]{2,1,0:T(8,128)(2,1)} %d_down.1, f32[8,128]{1,0:T(8,128)} %bitcast.8, ...), custom_call_target="tpu_custom_call" | custom-call | flops 62914560 | bytes 25165824 | tf_op jit(solution)/shard_map/send/pallas_call | solution.py:217
  8.8 82.0 %all_to_all.10.got.tile = bf16[16,1568,128]{2,1,0:T(8,128)(2,1)} all-to-all(bf16[16,1568,128]{2,1,0:T(8,128)(2,1)S(1)} %send.1), channel_id=1, replica_groups=mesh['owner'=8,'rows'=16] {'rows'}, dimensions={0} | all-to-all | bytes 12845056 | tf_op jit(solution)/shard_map/all_to_all | solution.py:277
  90.8 1.5 %copies.1 = bf16[8,8,2048]{2,1,0:T(8,128)(2,1)} custom-call(bf16[16,1568,128]{2,1,0:T(8,128)(2,1)} %all_to_all.10.got.tile), custom_call_target="tpu_custom_call" | custom-call | tf_op jit(solution)/shard_map/copies/pallas_call | solution.py:240
  92.3 6.5 %all-to-all-start.1 = ((bf16[8,8,2048]{2,1,0:T(8,128)(2,1)}), bf16[8,8,2048]{2,1,0:T(8,128)(2,1)S(1)}, u32[]{:S(2)}, u32[]{:S(2)}) async-start(bf16[8,8,2048]{2,1,0:T(8,128)(2,1)} %copies.1), calls=%async_computation.1 | async-start | bytes 524288 | tf_op jit(solution)/shard_map/all_to_all | solution.py:277
  98.8 7.7 %take.1 = (bf16[8,64,2048]{2,1,0:T(8,128)(2,1)}, bf16[8,64,2048]{2,1,0:T(8,128)(2,1)}, bf16[8,64,2048]{2,1,0:T(8,128)(2,1)}, f32[8,64]{1,0:T(8,128)}, f32[8,64]{1,0:T(8,128)}, /*index=5*/f32[8,64]{1,0:T(8,128)}) custom-call(bf16[16,1568,128]{2,1,0:T(8,128)(2,1)} %all_to_all.10.got.tile), custom_call_target="tpu_custom_call" | custom-call | flops 62914560 | bytes 25165824 | tf_op jit(solution)/shard_map/take/pallas_call | solution.py:253
  106.5 0.0 all-to-all-done.1
  106.5 0.7 copy.16
Async XLA Ops:
  92.3 14.2 %all-to-all-start.1 = ((bf16[8,8,2048]{2,1,0:T(8,128)(2,1)}), bf16[8,8,2048]{2,1,0:T(8,128)(2,1)S(1)}, u32[]{:S(2)}, u32[]{:S(2)}) async-start(bf16[8,8,2048]{2,1,0:T(8,128)(2,1)} %copies.1), calls=%async_computation.1 | async-start | bytes 524288 | tf_op jit(solution)/shard_map/all_to_all | solution.py:277
